TPU v7x, 512 devices: a whole 4x8x8 slice. The times are simulated.
512 devices in a mesh: front: 128 (over y, x, z_lo, core), sub: 4 (over z_hi).
Axes of the slice: x: 4, y: 8, z: 8 (z_hi: 4, z_lo: 2; z = z_hi * 2 + z_lo), core: 2. Of those that a mesh axis runs over, the one named last changes fastest.
Arguments:
- row_values: float32 [65536, 1024], P(('front', 'sub')), may hold values from -0.12 to 0.12
- front_of_row: int32 [65536, 1], P(('front', 'sub')), may hold values from 0 to 127; in each aligned block of 128 rows (0 to 127, 128 to 255, ...) at most 2 rows name the same one
- child_factors: float32 [256, 512, 512], P('front', 'sub'), as said below
- child_columns: int32 [256, 512], P('front'), may hold values from 0 to 1023, as said below
- damping: float32 [128, 1024], P('front'), may hold values from 0.5 to 2
Outputs:
- front_factor: float32 [128, 1024, 1024], P('front', 'sub')
Inputs may be any that keep to these rules, and one draw needn't show every extreme that they name: `front_of_row`: among the 128 rows of one device, at most 2 name the same front, and some device's block reaches this bound. `child_factors`: each block is upper triangular with a positive diagonal. `child_columns`: each row names 512 distinct columns.
All inputs are finite; a program needn't handle non-finite values.
Results may differ from a plain program's by a relative error of at most 0.0003.
Values sent between devices are 32-bit elements; how exact they have to be, the bound alone decides.
A program may use at most 64 MiB of HBM per device.

v0:
```python
import jax
import jax.numpy as jnp
from jax import lax
from jax.sharding import PartitionSpec as P

HIGHEST = lax.Precision.HIGHEST


def cross_product(left_cols, right_cols):
    return lax.dot_general(
        left_cols,
        right_cols,
        (((0,), (0,)), ((), ())),
        precision=HIGHEST,
        preferred_element_type=jnp.float32,
    )


def local(row_values, front_of_row, child_factors, child_columns, damping):
    fronts = lax.axis_size("front")
    rows_held, front_width = row_values.shape
    capacity = 2 * rows_held // fronts
    destination = front_of_row[:, 0]
    onehot = (destination[:, None] == jnp.arange(fronts, dtype=jnp.int32)[None, :]).astype(
        jnp.int32
    )
    position = jnp.sum((jnp.cumsum(onehot, axis=0) - onehot) * onehot, axis=1)
    slot_of = destination * capacity + position
    source = (
        jnp.full((fronts * capacity,), rows_held, jnp.int32)
        .at[slot_of]
        .set(jnp.arange(rows_held, dtype=jnp.int32))
    )
    padded = jnp.concatenate([row_values, jnp.zeros((1, front_width), row_values.dtype)], axis=0)
    outgoing = padded[source]
    received = lax.all_to_all(outgoing, "front", split_axis=0, concat_axis=0, tiled=True)
    columns = jnp.arange(front_width, dtype=jnp.int32)
    spread = (child_columns[:, :, None] == columns[None, None, :]).astype(jnp.float32)
    child_gram = jnp.einsum(
        "jrc,jrd->jcd",
        child_factors,
        child_factors,
        precision=HIGHEST,
        preferred_element_type=jnp.float32,
    )
    extended = jnp.einsum(
        "jcd,jdg->jcg", child_gram, spread, precision=HIGHEST, preferred_element_type=jnp.float32
    )
    sub_count = lax.axis_size("sub")
    block_rows = front_width // sub_count
    own_index = lax.axis_index("sub")
    weight = damping[0]
    child_part = jnp.einsum(
        "jcf,jcg->fg", spread, extended, precision=HIGHEST, preferred_element_type=jnp.float32
    )
    summed_gram = lax.psum(cross_product(received, received) + child_part, "sub")
    summed_gram = summed_gram + jnp.diag(weight * weight)
    full_factor = jnp.linalg.cholesky(summed_gram).T
    own_rows = lax.dynamic_slice_in_dim(full_factor, own_index * block_rows, block_rows, 0)
    return own_rows[None]


def solution(mesh):
    in_specs = (
        P(("front", "sub"), None),
        P(("front", "sub"), None),
        P("front", "sub", None),
        P("front", None),
        P("front", None),
    )
    out_specs = P("front", "sub", None)
    return jax.shard_map(local, mesh=mesh, in_specs=in_specs, out_specs=out_specs, check_vma=False)
```

profile of v0, /device:TPU:2, one launch (start us, length us, event | category | flops | bytes accessed | tf_op | source)
XLA Modules:
  0.0 471.8 jit_solution(10854724256641188840)
XLA Ops:
  13.8 13.2 %all-to-all-start = ((f32[128,2,1024]{2,1,0:T(2,128)}), f32[128,2,1024]{2,1,0:T(2,128)S(1)}, u32[]{:S(2)}, u32[]{:S(2)}) async-start(f32[128,2,1024]{2,1,0:T(2,128)} %all_to_all.6), calls=%async_computation | async-start | bytes 2097152 | tf_op jit(solution)/shard_map/all_to_all | solution.py:36
  29.1 3.8 fusion.2
  32.9 8.6 %fusion.1 = f32[1024,1024,1]{0,1,2:T(8,128)} fusion(f32[2,512,1024]{2,1,0:T(8,128)S(1)} %fusion.2, s32[2,512]{1,0:T(2,128)S(1)} %copy-done.3), kind=kOutput, calls=%fused_computation.8 | convolution fusion | flops 12885950464 | bytes 8392704 | tf_op jit(solution)/shard_map/jcf,jcg->fg/dot_general | solution.py:53
  41.5 15.6 %all-to-all-done = f32[128,2,1024]{2,1,0:T(2,128)S(1)} async-done(((f32[128,2,1024]{2,1,0:T(2,128)}), f32[128,2,1024]{2,1,0:T(2,128)S(1)}, u32[]{:S(2)}, u32[]{:S(2)}) %all-to-all-start) | async-done | bytes 1048608 | tf_op jit(solution)/shard_map/all_to_all | solution.py:36
  57.1 7.4 %bitcast_add_fusion.1 = f32[1024,1024]{0,1:T(8,128)} fusion(f32[1024,1024,1]{0,1,2:T(8,128)} %fusion.1, f32[128,2,1024]{2,1,0:T(2,128)S(1)} %all-to-all-done), kind=kOutput, calls=%fused_computation.4 | convolution fusion | flops 3222274048 | bytes 9437184 | tf_op jit(solution)/shard_map/dot_general | solution.py:10
  65.2 171.3 %all-reduce.4.cloned.1.call-done = f32[1024,1024]{0,1:T(8,128)} async-done(((f32[1024,1024]{0,1:T(8,128)}), f32[1024,1024]{0,1:T(8,128)}) %all-reduce.4.cloned.1.call-update) | async-done | bytes 4194320 | tf_op jit(solution)/shard_map/psum | solution.py:56
  236.5 4.8 %select_add_fusion = f32[1024,1024]{0,1:T(8,128)} fusion(f32[1024,1024]{0,1:T(8,128)} %all-reduce.4.cloned.1.call-done, f32[1024]{0:T(1024)S(1)} %bitcast.60), kind=kLoop, calls=%fused_computation.5 | loop fusion | flops 3145728 | bytes 8392704 | tf_op jit(solution)/shard_map/add | solution.py:57
  241.4 5.5 %copy.51 = f32[1024,1024]{1,0:T(8,128)} copy(f32[1024,1024]{0,1:T(8,128)} %select_add_fusion) | data formatting | bytes 8388608 | tf_op jit(solution)/shard_map/add | solution.py:57
  246.9 4.4 fusion
  253.3 11.7 %cholesky.224 = f32[128,128]{1,0:T(8,128)S(1)} custom-call(f32[128,128]{1,0:T(8,128)S(1)} %cholesky.580), custom_call_target="Cholesky" | custom-call | tf_op jit(solution)/shard_map/jit(cholesky)/cholesky | solution.py:58
  265.1 9.8 %custom-call.59 = f32[1,128,128]{1,2,0:T(8,128)S(1)} custom-call(f32[1,128,128]{2,1,0:T(8,128)S(1)} %get-tuple-element.18), custom_call_target="InvertDiagBlocksLowerTriangular" | custom-call | tf_op jit(solution)/shard_map/jit(cholesky)/cholesky | solution.py:58
  278.3 11.7 %cholesky.245 = f32[128,128]{1,0:T(8,128)S(1)} custom-call(f32[128,128]{1,0:T(8,128)S(1)} %cholesky.584), custom_call_target="Cholesky" | custom-call | tf_op jit(solution)/shard_map/jit(cholesky)/cholesky | solution.py:58
  293.0 9.8 %custom-call.60 = f32[1,128,128]{1,2,0:T(8,128)S(1)} custom-call(f32[1,128,128]{2,1,0:T(8,128)S(1)} %get-tuple-element.16), custom_call_target="InvertDiagBlocksLowerTriangular" | custom-call | tf_op jit(solution)/shard_map/jit(cholesky)/cholesky | solution.py:58
  308.3 11.7 %cholesky.469 = f32[128,128]{1,0:T(8,128)S(1)} custom-call(f32[128,128]{1,0:T(8,128)S(1)} %cholesky.589), custom_call_target="Cholesky" | custom-call | tf_op jit(solution)/shard_map/jit(cholesky)/cholesky | solution.py:58
  320.8 9.8 %custom-call.61 = f32[1,128,128]{1,2,0:T(8,128)S(1)} custom-call(f32[1,128,128]{2,1,0:T(8,128)S(1)} %get-tuple-element.14), custom_call_target="InvertDiagBlocksLowerTriangular" | custom-call | tf_op jit(solution)/shard_map/jit(cholesky)/cholesky | solution.py:58
  335.2 11.7 %cholesky.488 = f32[128,128]{1,0:T(8,128)S(1)} custom-call(f32[128,128]{1,0:T(8,128)S(1)} %cholesky.594), custom_call_target="Cholesky" | custom-call | tf_op jit(solution)/shard_map/jit(cholesky)/cholesky | solution.py:58
  347.7 9.8 %custom-call.62 = f32[1,128,128]{1,2,0:T(8,128)S(1)} custom-call(f32[1,128,128]{2,1,0:T(8,128)S(1)} %get-tuple-element.12), custom_call_target="InvertDiagBlocksLowerTriangular" | custom-call | tf_op jit(solution)/shard_map/jit(cholesky)/cholesky | solution.py:58
  361.8 11.9 %cholesky.507 = f32[128,128]{1,0:T(8,128)S(1)} custom-call(f32[128,128]{1,0:T(8,128)S(1)} %cholesky.599), custom_call_target="Cholesky" | custom-call | tf_op jit(solution)/shard_map/jit(cholesky)/cholesky | solution.py:58
  374.4 9.8 %custom-call.63 = f32[1,128,128]{1,2,0:T(8,128)S(1)} custom-call(f32[1,128,128]{2,1,0:T(8,128)S(1)} %get-tuple-element.10), custom_call_target="InvertDiagBlocksLowerTriangular" | custom-call | tf_op jit(solution)/shard_map/jit(cholesky)/cholesky | solution.py:58
  388.5 11.7 %cholesky.527 = f32[128,128]{1,0:T(8,128)S(1)} custom-call(f32[128,128]{1,0:T(8,128)S(1)} %cholesky.604), custom_call_target="Cholesky" | custom-call | tf_op jit(solution)/shard_map/jit(cholesky)/cholesky | solution.py:58
  400.9 9.8 %custom-call.64 = f32[1,128,128]{1,2,0:T(8,128)S(1)} custom-call(f32[1,128,128]{2,1,0:T(8,128)S(1)} %get-tuple-element.8), custom_call_target="InvertDiagBlocksLowerTriangular" | custom-call | tf_op jit(solution)/shard_map/jit(cholesky)/cholesky | solution.py:58
  414.7 11.7 %cholesky.547 = f32[128,128]{1,0:T(8,128)S(1)} custom-call(f32[128,128]{1,0:T(8,128)S(1)} %cholesky.609), custom_call_target="Cholesky" | custom-call | tf_op jit(solution)/shard_map/jit(cholesky)/cholesky | solution.py:58
  427.2 9.8 %custom-call.65 = f32[1,128,128]{1,2,0:T(8,128)S(1)} custom-call(f32[1,128,128]{2,1,0:T(8,128)S(1)} %get-tuple-element.6), custom_call_target="InvertDiagBlocksLowerTriangular" | custom-call | tf_op jit(solution)/shard_map/jit(cholesky)/cholesky | solution.py:58
  440.0 11.7 %cholesky.565 = f32[128,128]{1,0:T(8,128)S(1)} custom-call(f32[128,128]{1,0:T(8,128)S(1)} %convolution_subtract_fusion.6), custom_call_target="Cholesky" | custom-call | tf_op jit(solution)/shard_map/jit(cholesky)/cholesky | solution.py:58
  (78 shorter events, 55.0 us)
Async XLA Ops:
  6.5 20.7 %copy-start = (f32[2,128,512]{2,1,0:T(8,128)S(1)}, f32[2,128,512]{2,1,0:T(8,128)}, u32[]{:S(2)}) copy-start(f32[2,128,512]{2,1,0:T(8,128)} %param.7) | copy-start | bytes 1572868
  12.2 16.9 %copy-start.3 = (s32[2,512]{1,0:T(2,128)S(1)}, s32[2,512]{1,0:T(2,128)}, u32[]{:S(2)}) copy-start(s32[2,512]{1,0:T(2,128)} %param.8) | copy-start | bytes 12292
  13.8 43.3 %all-to-all-start = ((f32[128,2,1024]{2,1,0:T(2,128)}), f32[128,2,1024]{2,1,0:T(2,128)S(1)}, u32[]{:S(2)}, u32[]{:S(2)}) async-start(f32[128,2,1024]{2,1,0:T(2,128)} %all_to_all.6), calls=%async_computation | async-start | bytes 2097152 | tf_op jit(solution)/shard_map/all_to_all | solution.py:36
  27.0 209.5 %all-reduce.4.cloned.1.call-start = ((), (), s32[]{:S(2)}) async-start(), calls=%async_computation.1 | async-start | bytes 8388608 | tf_op jit(solution)/shard_map/psum | solution.py:56
  64.5 0.7 copy-start.2
  251.3 1.9 copy-start.1
Sparse Core Ops, SparseCore 0:
  64.7 171.7 all-reduce.3
where the time goes:
time: 476 us; the launch traced here: 472 us
  waiting for transfers between devices  187 us (39%)
  other arithmetic  182 us (38%)
  matrix products  48.7 us (10%)
  local copies, waits for them, and re-layouts  21.6 us (5%)
  between operations  19.5 us (4%)
  starting transfers between devices  13.5 us (3%)
    psum x1, waiting for transfers between devices, local(): lax.psum(cross_product(received, received) + child_part, 'sub')  171 us
    another operation x30, other arithmetic, local(): full_factor = jnp.linalg.cholesky(summed_gram).T  167 us
    another operation x14, matrix products, local(): full_factor = jnp.linalg.cholesky(summed_gram).T  27 us
    all_to_all x1, waiting for transfers between devices, local(): lax.all_to_all(outgoing, 'front', split_axis=0, concat_axis=0, tiled=True)  15.6 us
    all_to_all x1, starting transfers between devices, local(): lax.all_to_all(outgoing, 'front', split_axis=0, concat_axis=0, tiled=True)  13.2 us
  transfers between devices with their start and end apart: 2, of which 2 were waited for; matrix products, arithmetic and copies ran while one was open for 3% of the time, Pallas kernels for 0%

commit v1 on v0

v1 whole, which is shorter than its diff:
```python
import jax
import jax.numpy as jnp
from jax import lax
from jax.experimental import pallas as pl
from jax.experimental.pallas import tpu as pltpu
from jax.sharding import PartitionSpec as P

F32 = jnp.float32
BF16 = jnp.bfloat16
BLOCK = 128
LANES = 128
GROUP = 8
MESH = pl.DeviceIdType.MESH
KEEP = (((1,), (0,)), ((), ()))
ROWS = (((0,), (0,)), ((), ()))
COLS = (((1,), (1,)), ((), ()))


def mm(left, right, dims):
    return lax.dot_general(left, right, dims, preferred_element_type=F32)


def split(x):
    high = x.astype(BF16)
    return high, (x - high.astype(F32)).astype(BF16)


def mm3(left, right, dims):
    return mm(left[0], right[0], dims) + (mm(left[0], right[1], dims) + mm(left[1], right[0], dims))


def root_of(front):
    return 2 * (front % 2) + (front // 2) % 2


def exchange_kernel(fronts, subs, rows_ref, dest_ref, child_ref, recv_ref, children_ref, slots, own_sem, send_sem, child_send, recv_sem, child_sem):
    me = lax.axis_index("front")
    sub = lax.axis_index("sub")
    rows_held = rows_ref.shape[0]
    root = root_of(me)
    chosen = (dest_ref[...] == lax.broadcasted_iota(jnp.int32, (rows_held, fronts), 1)).astype(F32)
    before = (
        lax.broadcasted_iota(jnp.int32, (rows_held, rows_held), 1)
        < lax.broadcasted_iota(jnp.int32, (rows_held, rows_held), 0)
    ).astype(BF16)
    earlier = mm(before, chosen.astype(BF16), KEEP)
    parts = split(rows_ref[...])
    per_row = rows_ref.shape[1] // LANES
    for slot in range(2):
        pick = jnp.where(earlier == slot, chosen, 0.0).astype(BF16)
        placed = mm(pick, parts[0], ROWS) + mm(pick, parts[1], ROWS)
        for k in range(per_row):
            slots[pl.ds(slot * per_row + k, fronts, stride=2 * per_row), :] = placed[:, k * LANES : (k + 1) * LANES]

    size = 2 * per_row
    mine = me * subs + sub

    def piece(front):
        return slots.at[pl.ds(pl.multiple_of(front * size, size), size), :]

    def child_copy(s):
        return pltpu.make_async_remote_copy(
            src_ref=child_ref.at[:, :, s * BLOCK :],
            dst_ref=children_ref.at[s, :, :, s * BLOCK :],
            send_sem=child_send,
            recv_sem=child_sem.at[s],
            device_id=(me, root),
            device_id_type=MESH,
        )

    for s in range(subs):

        @pl.when((sub == s) & (root != s))
        def _():
            child_copy(s).start()

    def send(i, carry):
        front = lax.rem(me + i, fronts)
        target = root_of(front)

        @pl.when((front != me) | (target != sub))
        def _():
            pltpu.make_async_remote_copy(
                src_ref=piece(front),
                dst_ref=recv_ref.at[mine],
                send_sem=send_sem,
                recv_sem=recv_sem,
                device_id=(front, target),
                device_id_type=MESH,
            ).start()

        return carry

    lax.fori_loop(0, fronts, send, 0)
    for s in range(subs):

        @pl.when((sub == s) & (root == s))
        def _():
            own = pltpu.make_async_copy(piece(me), recv_ref.at[mine], own_sem.at[0])
            own.start()
            kids = pltpu.make_async_copy(
                child_ref.at[:, :, s * BLOCK :], children_ref.at[s, :, :, s * BLOCK :], own_sem.at[1]
            )
            kids.start()
            own.wait()
            kids.wait()
            everyone = recv_ref.at[pl.ds(0, fronts * subs - 1)]
            pltpu.make_async_copy(everyone, everyone, recv_sem).wait()
            for other in range(subs):
                if other != s:
                    child_copy(other).wait_recv()
            sent = slots.at[pl.ds(0, (fronts - 1) * size), :]
            pltpu.make_async_copy(sent, sent, send_sem).wait()

        @pl.when((sub == s) & (root != s))
        def _():
            child_copy(s).wait_send()
            pltpu.make_async_copy(slots, slots, send_sem).wait()


def exchange(rows, dest, child, fronts, subs):
    rows_held, width = rows.shape
    per_row = width // LANES
    size = 2 * per_row
    return pl.pallas_call(
        lambda *refs: exchange_kernel(fronts, subs, *refs),
        out_shape=[
            jax.ShapeDtypeStruct((fronts * subs, size, LANES), F32),
            jax.ShapeDtypeStruct((subs,) + child.shape, F32),
        ],
        in_specs=[
            pl.BlockSpec(memory_space=pltpu.VMEM),
            pl.BlockSpec(memory_space=pltpu.VMEM),
            pl.BlockSpec(memory_space=pl.ANY),
        ],
        out_specs=[pl.BlockSpec(memory_space=pl.ANY)] * 2,
        scratch_shapes=[
            pltpu.VMEM((fronts * size, LANES), F32),
            pltpu.SemaphoreType.DMA((2,)),
            pltpu.SemaphoreType.DMA,
            pltpu.SemaphoreType.DMA,
            pltpu.SemaphoreType.DMA,
            pltpu.SemaphoreType.DMA((subs,)),
        ],
        compiler_params=pltpu.CompilerParams(has_side_effects=True),
        name="ray_exchange",
    )(rows, dest, child)


def lane_copy(x, j):
    return jnp.broadcast_to(x[:, j : j + 1], (GROUP, LANES))


def row_copy(x, j):
    return jnp.broadcast_to(x[j : j + 1, :], (GROUP, LANES))


def factor_block(source, upper_ref, inverse_ref):
    count = BLOCK // GROUP
    sub = lax.broadcasted_iota(jnp.int32, (GROUP, LANES), 0)
    lane = lax.broadcasted_iota(jnp.int32, (GROUP, LANES), 1)
    a = [source[GROUP * k : GROUP * (k + 1), :] for k in range(count)]
    e = [jnp.where(lane == sub + GROUP * k, 1.0, 0.0).astype(F32) for k in range(count)]
    for k in range(count):
        b = [lane_copy(a[k], GROUP * k + m) for m in range(GROUP)]
        pivots = None
        u = [[None] * GROUP for _ in range(GROUP)]
        inv = [None] * GROUP
        for j in range(GROUP):
            pivot = row_copy(b[j], j)
            pivots = pivot if pivots is None else jnp.where(sub >= j, pivot, pivots)
            inv[j] = 1.0 / pivot
            ratio = jnp.where(sub > j, b[j], 0.0) * inv[j]
            for m in range(j + 1, GROUP):
                u[j][m] = row_copy(b[m], j)
                b[m] = b[m] - ratio * u[j][m]
            a[k] = a[k] - ratio * row_copy(a[k], j)
            e[k] = e[k] - ratio * row_copy(e[k], j)
        scale = lax.rsqrt(pivots)
        upper_ref[GROUP * k : GROUP * (k + 1), :] = a[k] * scale
        inverse_ref[GROUP * k : GROUP * (k + 1), :] = e[k] * scale
        rows_a = [row_copy(a[k], j) for j in range(GROUP)]
        rows_e = [row_copy(e[k], j) for j in range(GROUP)]
        for q in range(k + 1, count):
            c = [lane_copy(a[q], GROUP * k + m) for m in range(GROUP)]
            for j in range(GROUP):
                ratio = c[j] * inv[j]
                for m in range(j + 1, GROUP):
                    c[m] = c[m] - ratio * u[j][m]
                a[q] = a[q] - ratio * rows_a[j]
                e[q] = e[q] - ratio * rows_e[j]


def factor_kernel(recv_ref, children_ref, columns_ref, damping_ref, r_ref, xh, xl, rh, rl, panel, block, upper, inverse):
    width = r_ref.shape[1]
    per_row = width // LANES
    rays = recv_ref.shape[0] // per_row
    subs, kids, _, contrib = children_ref.shape
    me = lax.axis_index("front")
    sub = lax.axis_index("sub")

    @pl.when(sub == root_of(me))
    def _():
        def take(i, carry):
            base = pl.multiple_of(i * BLOCK, BLOCK)
            for k in range(per_row):
                high, low = split(recv_ref[pl.ds(base * per_row + k, BLOCK, stride=per_row), :])
                xh[pl.ds(base, BLOCK), k * LANES : (k + 1) * LANES] = high
                xl[pl.ds(base, BLOCK), k * LANES : (k + 1) * LANES] = low
            return carry

        lax.fori_loop(0, rays // BLOCK, take, 0)
        for c in range(kids):
            spread = (
                lax.broadcasted_iota(jnp.int32, (width, contrib), 0) == columns_ref[c : c + 1, :]
            ).astype(F32).astype(BF16)
            for s in range(subs):
                high, low = split(children_ref[s, c, :, s * BLOCK :])
                at = rays + c * contrib + s * BLOCK
                xh[at : at + BLOCK, :] = mm(high, spread[:, s * BLOCK :], COLS).astype(BF16)
                xl[at : at + BLOCK, :] = mm(low, spread[:, s * BLOCK :], COLS).astype(BF16)
        on_diagonal = lax.broadcasted_iota(jnp.int32, (BLOCK, BLOCK), 0) == lax.broadcasted_iota(
            jnp.int32, (BLOCK, BLOCK), 1
        )

        def step(i, carry):
            for b in range(width // BLOCK):

                @pl.when(i == b)
                def _():
                    c0, c1 = b * BLOCK, (b + 1) * BLOCK
                    acc = mm3((xh[:, c0:c1], xl[:, c0:c1]), (xh[:, c0:], xl[:, c0:]), ROWS)
                    if b:
                        acc = acc - mm3((rh[:c0, c0:c1], rl[:c0, c0:c1]), (rh[:c0, c0:], rl[:c0, c0:]), ROWS)
                    panel[:, c0:] = acc
                    weight = damping_ref[:, c0:c1]
                    block[...] = acc[:, :BLOCK] + jnp.where(on_diagonal, weight * weight, 0.0)

            factor_block(block, upper, inverse)
            for b in range(width // BLOCK):

                @pl.when(i == b)
                def _():
                    c0, c1 = b * BLOCK, (b + 1) * BLOCK
                    if b:
                        r_ref[c0:c1, :c0] = jnp.zeros((BLOCK, c0), F32)
                    r_ref[c0:c1, c0:c1] = upper[...]
                    if c1 < width:
                        rest = mm3(split(inverse[...]), split(panel[:, c1:]), KEEP)
                        r_ref[c0:c1, c1:] = rest
                        rh[c0:c1, c1:], rl[c0:c1, c1:] = split(rest)

            return carry

        lax.fori_loop(0, width // BLOCK, step, 0)


def factor(recv, children, columns, damping):
    width = damping.shape[1]
    total = recv.shape[0] * LANES // width + children.shape[1] * children.shape[3]
    return pl.pallas_call(
        factor_kernel,
        out_shape=jax.ShapeDtypeStruct((width, width), F32),
        in_specs=[pl.BlockSpec(memory_space=pltpu.VMEM)] * 4,
        out_specs=pl.BlockSpec(memory_space=pltpu.VMEM),
        scratch_shapes=[
            pltpu.VMEM((total, width), BF16),
            pltpu.VMEM((total, width), BF16),
            pltpu.VMEM((width, width), BF16),
            pltpu.VMEM((width, width), BF16),
            pltpu.VMEM((BLOCK, width), F32),
            pltpu.VMEM((BLOCK, BLOCK), F32),
            pltpu.VMEM((BLOCK, BLOCK), F32),
            pltpu.VMEM((BLOCK, BLOCK), F32),
        ],
        name="front_factor",
    )(recv, children, columns, damping)


def spread_kernel(subs, r_ref, out_ref, send_sem, recv_sem, own_sem):
    me = lax.axis_index("front")
    sub = lax.axis_index("sub")
    root = root_of(me)
    rows = out_ref.shape[0]
    barrier = pltpu.get_barrier_semaphore()

    @pl.when(sub != root)
    def _():
        pl.semaphore_signal(barrier, inc=1, device_id=(me, root), device_id_type=MESH)

    @pl.when(sub == root)
    def _():
        pl.semaphore_wait(barrier, subs - 1)

    def copy(s):
        return pltpu.make_async_remote_copy(
            src_ref=r_ref.at[s * rows : (s + 1) * rows, :],
            dst_ref=out_ref,
            send_sem=send_sem.at[s],
            recv_sem=recv_sem,
            device_id=(me, s),
            device_id_type=MESH,
        )

    for r in range(subs):

        @pl.when((sub == r) & (root == r))
        def _():
            for s in range(subs):
                if s != r:
                    copy(s).start()
            own = pltpu.make_async_copy(r_ref.at[r * rows : (r + 1) * rows, :], out_ref, own_sem)
            own.start()
            own.wait()
            for s in range(subs):
                if s != r:
                    copy(s).wait_send()

        @pl.when((sub == r) & (root != r))
        def _():
            copy(r).wait_recv()


def spread_rows(r, subs):
    width = r.shape[0]
    return pl.pallas_call(
        lambda *refs: spread_kernel(subs, *refs),
        out_shape=jax.ShapeDtypeStruct((width // subs, width), F32),
        in_specs=[pl.BlockSpec(memory_space=pl.ANY)],
        out_specs=pl.BlockSpec(memory_space=pl.ANY),
        scratch_shapes=[
            pltpu.SemaphoreType.DMA((subs,)),
            pltpu.SemaphoreType.DMA,
            pltpu.SemaphoreType.DMA,
        ],
        compiler_params=pltpu.CompilerParams(collective_id=1, has_side_effects=True),
        name="factor_rows_out",
    )(r)


def local(row_values, front_of_row, child_factors, child_columns, damping):
    fronts = lax.axis_size("front")
    subs = lax.axis_size("sub")
    recv, children = exchange(row_values, front_of_row, child_factors, fronts, subs)
    recv = recv.reshape((-1, LANES))
    r = factor(recv, children, child_columns, damping)
    return spread_rows(r, subs)[None]


def solution(mesh):
    in_specs = (
        P(("front", "sub"), None),
        P(("front", "sub"), None),
        P("front", "sub", None),
        P("front", None),
        P("front", None),
    )
    out_specs = P("front", "sub", None)
    return jax.shard_map(local, mesh=mesh, in_specs=in_specs, out_specs=out_specs, check_vma=False)
```

time: 476 us -> 169 us (0.36)
  the two profiles are of different devices: /device:TPU:2 before, /device:TPU:8 now
where the time goes in v1:
time: 169 us
  Pallas kernels  165 us (98%)
  local copies, waits for them, and re-layouts  3.7 us (2%)
    pallas_call x1, Pallas kernels, exchange(): pl.pallas_call(lambda *refs: exchange_kernel(fronts, subs, *refs), out_sh...  72.8 us
    pallas_call x1, Pallas kernels, factor(): pl.pallas_call(factor_kernel, out_shape=jax.ShapeDtypeStruct((width, widt...  56.8 us
    pallas_call x1, Pallas kernels, spread_rows(): pl.pallas_call(lambda *refs: spread_kernel(subs, *refs), out_shape=jax.Sh...  35.9 us
    unnamed x2, local copies, waits for them, and re-layouts  3.7 us

profile of v1, /device:TPU:8, one launch (start us, length us, event | category | flops | bytes accessed | tf_op | source)
XLA Modules:
  0.0 169.2 jit_solution(3254940012725424989)
XLA Ops:
  0.0 1.4 copy.6.refs_1_
  1.4 72.8 %ray_exchange.1 = (f32[512,16,128]{2,1,0:T(8,128)}, f32[4,2,128,512]{3,2,1,0:T(8,128)}) custom-call(f32[128,1024]{1,0:T(8,128)} %refs_0_.1, s32[128,1]{1,0:T(8,128)} %copy.6.refs_1_, f32[2,128,512]{2,1,0:T(8,128)} %refs_2_.1), custom_call_target="tpu_custom_call" | custom-call | tf_op jit(solution)/shard_map/ray_exchange/pallas_call | solution.py:125
  74.2 56.8 %front_factor.1.refs_0_ = f32[1024,1024]{1,0:T(8,128)} custom-call(f32[8192,128]{1,0:T(8,128)} %bitcast.3, f32[4,2,128,512]{3,2,1,0:T(8,128)} %get-tuple-element.8.children_ref, s32[2,512]{1,0:T(2,128)} %columns_ref.1, f32[1,1024]{1,0:T(1,128)} %damping_ref.1), custom_call_target="tpu_custom_call" | custom-call | tf_op jit(solution)/shard_map/front_factor/pallas_call | solution.py:261
  131.0 35.9 %factor_rows_out.1 = f32[256,1024]{1,0:T(8,128)} custom-call(f32[1024,1024]{1,0:T(8,128)} %front_factor.1.refs_0_), custom_call_target="tpu_custom_call" | custom-call | tf_op jit(solution)/shard_map/factor_rows_out/pallas_call | solution.py:326
  166.9 2.3 %copy.8 = f32[1,256,1024]{2,1,0:T(8,128)} copy(f32[1,256,1024]{2,1,0:T(8,128)} %bitcast.2) | data formatting | bytes 2097152

commit v2 on v0

v2 whole, which is shorter than its diff:
```python
import jax
import jax.numpy as jnp
from jax import lax
from jax.experimental import pallas as pl
from jax.experimental.pallas import tpu as pltpu
from jax.sharding import PartitionSpec as P

F32 = jnp.float32
BF16 = jnp.bfloat16
BLOCK = 128
LANES = 128
GROUP = 8
GROUPS = 4
STRIDE = 53
MESH = pl.DeviceIdType.MESH
KEEP = (((1,), (0,)), ((), ()))
ROWS = (((0,), (0,)), ((), ()))
COLS = (((1,), (1,)), ((), ()))


def mm(left, right, dims):
    return lax.dot_general(left, right, dims, preferred_element_type=F32)


def split(x):
    high = x.astype(BF16)
    return high, (x - high.astype(F32)).astype(BF16)


def mm3(left, right, dims):
    return mm(left[0], right[0], dims) + (mm(left[0], right[1], dims) + mm(left[1], right[0], dims))


def root_of(front):
    return lax.rem(2 * (front % 2) + (front // 2) % 2 + front // 4 + front // 16, 4)


def lane_copy(x, j):
    return jnp.broadcast_to(x[:, j : j + 1], (GROUP, LANES))


def row_copy(x, j):
    return jnp.broadcast_to(x[j : j + 1, :], (GROUP, LANES))


def factor_block(source, upper_ref, inverse_ref):
    count = BLOCK // GROUP
    sub = lax.broadcasted_iota(jnp.int32, (GROUP, LANES), 0)
    lane = lax.broadcasted_iota(jnp.int32, (GROUP, LANES), 1)
    a = [source[GROUP * k : GROUP * (k + 1), :] for k in range(count)]
    e = [jnp.where(lane == sub + GROUP * k, 1.0, 0.0).astype(F32) for k in range(count)]
    for k in range(count):
        b = [lane_copy(a[k], GROUP * k + m) for m in range(GROUP)]
        pivots = None
        u = [[None] * GROUP for _ in range(GROUP)]
        inv = [None] * GROUP
        for j in range(GROUP):
            pivot = row_copy(b[j], j)
            pivots = pivot if pivots is None else jnp.where(sub >= j, pivot, pivots)
            inv[j] = 1.0 / pivot
            ratio = jnp.where(sub > j, b[j], 0.0) * inv[j]
            for m in range(j + 1, GROUP):
                u[j][m] = row_copy(b[m], j)
                b[m] = b[m] - ratio * u[j][m]
            a[k] = a[k] - ratio * row_copy(a[k], j)
            e[k] = e[k] - ratio * row_copy(e[k], j)
        scale = lax.rsqrt(pivots)
        upper_ref[GROUP * k : GROUP * (k + 1), :] = a[k] * scale
        inverse_ref[GROUP * k : GROUP * (k + 1), :] = e[k] * scale
        rows_a = [row_copy(a[k], j) for j in range(GROUP)]
        rows_e = [row_copy(e[k], j) for j in range(GROUP)]
        for q in range(k + 1, count):
            c = [lane_copy(a[q], GROUP * k + m) for m in range(GROUP)]
            for j in range(GROUP):
                ratio = c[j] * inv[j]
                for m in range(j + 1, GROUP):
                    c[m] = c[m] - ratio * u[j][m]
                a[q] = a[q] - ratio * rows_a[j]
                e[q] = e[q] - ratio * rows_e[j]


def merge_kernel(
    fronts,
    subs,
    rows_ref,
    dest_ref,
    child_ref,
    columns_ref,
    damping_ref,
    out_ref,
    slots,
    recv,
    children,
    zeros,
    xh,
    xl,
    gram,
    r_full,
    rh,
    rl,
    block,
    upper,
    inverse,
    send_sem,
    recv_sem,
    child_send,
    child_recv,
    child_own,
    fill_sem,
    row_send,
    row_recv,
):
    me = lax.axis_index("front")
    sub = lax.axis_index("sub")
    root = root_of(me)
    rows_held, width = rows_ref.shape
    kids, _, contrib = child_ref.shape
    per_row = width // LANES
    size = 2 * per_row
    groups = recv_sem.shape[0]
    blocks = width // BLOCK
    per_sub = blocks // subs

    def child_copy(s):
        return pltpu.make_async_remote_copy(
            src_ref=child_ref.at[:, :, s * BLOCK :],
            dst_ref=children.at[s, :, :, s * BLOCK :],
            send_sem=child_send,
            recv_sem=child_recv.at[s],
            device_id=(me, root),
            device_id_type=MESH,
        )

    def child_keep(s):
        return pltpu.make_async_copy(child_ref.at[:, :, s * BLOCK :], children.at[s, :, :, s * BLOCK :], child_own)

    for s in range(subs):

        @pl.when((sub == s) & (root != s))
        def _():
            child_copy(s).start()

        @pl.when((sub == s) & (root == s))
        def _():
            child_keep(s).start()

    def fill(b):
        half = b % per_sub
        return pltpu.make_async_copy(
            zeros.at[:, : b * BLOCK], out_ref.at[half * BLOCK : (half + 1) * BLOCK, : b * BLOCK], fill_sem.at[half]
        )

    zeros[...] = jnp.zeros_like(zeros)

    chosen = (dest_ref[...] == lax.broadcasted_iota(jnp.int32, (rows_held, fronts), 1)).astype(F32)
    before = (
        lax.broadcasted_iota(jnp.int32, (rows_held, rows_held), 1)
        < lax.broadcasted_iota(jnp.int32, (rows_held, rows_held), 0)
    ).astype(BF16)
    earlier = mm(before, chosen.astype(BF16), KEEP)
    parts = split(rows_ref[...])
    for slot in range(2):
        pick = jnp.where(earlier == slot, chosen, 0.0).astype(BF16)
        placed = mm(pick, parts[0], ROWS) + mm(pick, parts[1], ROWS)
        for k in range(per_row):
            slots[pl.ds(slot * per_row + k, fronts, stride=size), :] = placed[:, k * LANES : (k + 1) * LANES]

    def piece(front):
        return slots.at[pl.ds(pl.multiple_of(front * size, size), size), :]

    steps = fronts // groups
    for g in range(groups):

        def send(i, carry):
            front = lax.rem(me + STRIDE * i, fronts)
            target = root_of(front)

            @pl.when((front != me) | (target != sub))
            def _():
                pltpu.make_async_remote_copy(
                    src_ref=piece(front),
                    dst_ref=recv.at[pl.ds(pl.multiple_of((i * subs + sub) * size, size), size), :],
                    send_sem=send_sem,
                    recv_sem=recv_sem.at[g],
                    device_id=(front, target),
                    device_id_type=MESH,
                ).start()

            return carry

        lax.fori_loop(g * steps, (g + 1) * steps, send, 0)

    for b in range(blocks):
        if b:

            @pl.when(sub == b // per_sub)
            def _():
                fill(b).start()

    def row_copy_out(b):
        half = b % per_sub
        return pltpu.make_async_remote_copy(
            src_ref=r_full.at[b * BLOCK : (b + 1) * BLOCK, b * BLOCK :],
            dst_ref=out_ref.at[half * BLOCK : (half + 1) * BLOCK, b * BLOCK :],
            send_sem=row_send.at[b],
            recv_sem=row_recv.at[half],
            device_id=(me, b // per_sub),
            device_id_type=MESH,
        )

    def row_keep(b):
        half = b % per_sub
        return pltpu.make_async_copy(
            r_full.at[b * BLOCK : (b + 1) * BLOCK, b * BLOCK :],
            out_ref.at[half * BLOCK : (half + 1) * BLOCK, b * BLOCK :],
            row_send.at[b],
        )

    @pl.when(sub == root)
    def _():
        recv[pl.ds(pl.multiple_of(sub * size, size), size), :] = slots[pl.ds(pl.multiple_of(me * size, size), size), :]
        for s in range(subs):

            @pl.when(root == s)
            def _():
                child_keep(s).wait()

            @pl.when(root != s)
            def _():
                child_copy(s).wait_recv()

        for c in range(kids):
            spread = (
                lax.broadcasted_iota(jnp.int32, (width, contrib), 0) == columns_ref[c : c + 1, :]
            ).astype(F32).astype(BF16)
            for s in range(subs):
                high, low = split(children[s, c, :, s * BLOCK :])
                at = c * contrib + s * BLOCK
                xh[at : at + BLOCK, :] = mm(high, spread[:, s * BLOCK :], COLS).astype(BF16)
                xl[at : at + BLOCK, :] = mm(low, spread[:, s * BLOCK :], COLS).astype(BF16)
        on_diagonal = lax.broadcasted_iota(jnp.int32, (BLOCK, BLOCK), 0) == lax.broadcasted_iota(
            jnp.int32, (BLOCK, BLOCK), 1
        )
        for b in range(blocks):
            c0, c1 = b * BLOCK, (b + 1) * BLOCK
            gram[c0:c1, c0:] = mm3((xh[:, c0:c1], xl[:, c0:c1]), (xh[:, c0:], xl[:, c0:]), ROWS)
            weight = damping_ref[:, c0:c1]
            gram[c0:c1, c0:c1] += jnp.where(on_diagonal, weight * weight, 0.0)

        slots_in = steps * subs
        count = 2 * slots_in

        def gather(g, carry):
            for h in range(groups):

                @pl.when(g == h)
                def _():
                    first = 1 if h == 0 else 0
                    region = recv.at[pl.ds(0, (slots_in - first) * size), :]
                    pltpu.make_async_copy(region, region, recv_sem.at[h]).wait()

            for q in range(count // BLOCK):
                base = pl.multiple_of(g * count + q * BLOCK, BLOCK)
                for k in range(per_row):
                    high, low = split(recv[pl.ds(base * per_row + k, BLOCK, stride=per_row), :])
                    xh[q * BLOCK : (q + 1) * BLOCK, k * LANES : (k + 1) * LANES] = high
                    xl[q * BLOCK : (q + 1) * BLOCK, k * LANES : (k + 1) * LANES] = low
            for b in range(blocks):
                c0, c1 = b * BLOCK, (b + 1) * BLOCK
                gram[c0:c1, c0:] += mm3(
                    (xh[:count, c0:c1], xl[:count, c0:c1]), (xh[:count, c0:], xl[:count, c0:]), ROWS
                )
            return carry

        lax.fori_loop(0, groups, gather, 0)

        def step(i, carry):
            for b in range(blocks):

                @pl.when(i == b)
                def _():
                    c0, c1 = b * BLOCK, (b + 1) * BLOCK
                    if b:
                        gram[c0:c1, c0:] -= mm3(
                            (rh[:c0, c0:c1], rl[:c0, c0:c1]), (rh[:c0, c0:], rl[:c0, c0:]), ROWS
                        )
                    block[...] = gram[c0:c1, c0:c1]

            factor_block(block, upper, inverse)
            for b in range(blocks):

                @pl.when(i == b)
                def _():
                    c0, c1 = b * BLOCK, (b + 1) * BLOCK
                    r_full[c0:c1, c0:c1] = upper[...]
                    if c1 < width:
                        rest = mm3(split(inverse[...]), split(gram[c0:c1, c1:]), KEEP)
                        r_full[c0:c1, c1:] = rest
                        rh[c0:c1, c1:], rl[c0:c1, c1:] = split(rest)

                    @pl.when(root != b // per_sub)
                    def _():
                        row_copy_out(b).start()

                    @pl.when(root == b // per_sub)
                    def _():
                        row_keep(b).start()

            return carry

        lax.fori_loop(0, blocks, step, 0)
        for b in range(blocks):

            @pl.when(root != b // per_sub)
            def _():
                row_copy_out(b).wait_send()

            @pl.when(root == b // per_sub)
            def _():
                row_keep(b).wait()

        sent = slots.at[pl.ds(0, (fronts - 1) * size), :]
        pltpu.make_async_copy(sent, sent, send_sem).wait()

    @pl.when(sub != root)
    def _():
        for s in range(subs):

            @pl.when(sub == s)
            def _():
                child_copy(s).wait_send()
                for b in range(s * per_sub, (s + 1) * per_sub):
                    row_copy_out(b).wait_recv()

        pltpu.make_async_copy(slots, slots, send_sem).wait()

    for b in range(blocks):
        if b:

            @pl.when(sub == b // per_sub)
            def _():
                fill(b).wait()


def merge(rows, dest, child, columns, damping, fronts, subs):
    rows_held, width = rows.shape
    size = 2 * width // LANES
    kids, _, contrib = child.shape
    groups = GROUPS
    deep = max(kids * contrib, 2 * fronts * subs // groups)
    blocks = width // BLOCK
    vmem = pl.BlockSpec(memory_space=pltpu.VMEM)
    return pl.pallas_call(
        lambda *refs: merge_kernel(fronts, subs, *refs),
        out_shape=jax.ShapeDtypeStruct((width // subs, width), F32),
        in_specs=[vmem, vmem, pl.BlockSpec(memory_space=pl.ANY), vmem, vmem],
        out_specs=pl.BlockSpec(memory_space=pl.ANY),
        scratch_shapes=[
            pltpu.VMEM((fronts * size, LANES), F32),
            pltpu.VMEM((fronts * subs * size, LANES), F32),
            pltpu.VMEM((subs,) + child.shape, F32),
            pltpu.VMEM((BLOCK, width), F32),
            pltpu.VMEM((deep, width), BF16),
            pltpu.VMEM((deep, width), BF16),
            pltpu.VMEM((width, width), F32),
            pltpu.VMEM((width, width), F32),
            pltpu.VMEM((width, width), BF16),
            pltpu.VMEM((width, width), BF16),
            pltpu.VMEM((BLOCK, BLOCK), F32),
            pltpu.VMEM((BLOCK, BLOCK), F32),
            pltpu.VMEM((BLOCK, BLOCK), F32),
            pltpu.SemaphoreType.DMA,
            pltpu.SemaphoreType.DMA((groups,)),
            pltpu.SemaphoreType.DMA,
            pltpu.SemaphoreType.DMA((subs,)),
            pltpu.SemaphoreType.DMA,
            pltpu.SemaphoreType.DMA((blocks // subs,)),
            pltpu.SemaphoreType.DMA((blocks,)),
            pltpu.SemaphoreType.DMA((blocks // subs,)),
        ],
        compiler_params=pltpu.CompilerParams(has_side_effects=True),
        name="front_merge",
    )(rows, dest, child, columns, damping)


def local(row_values, front_of_row, child_factors, child_columns, damping):
    fronts = lax.axis_size("front")
    subs = lax.axis_size("sub")
    return merge(row_values, front_of_row, child_factors, child_columns, damping, fronts, subs)[None]


def solution(mesh):
    in_specs = (
        P(("front", "sub"), None),
        P(("front", "sub"), None),
        P("front", "sub", None),
        P("front", None),
        P("front", None),
    )
    out_specs = P("front", "sub", None)
    return jax.shard_map(local, mesh=mesh, in_specs=in_specs, out_specs=out_specs, check_vma=False)
```

time: 476 us -> 115 us (0.24)
  the two profiles are of different devices: /device:TPU:2 before, /device:TPU:11 now
where the time goes in v2:
time: 115 us
  Pallas kernels  112 us (97%)
  local copies, waits for them, and re-layouts  3.7 us (3%)
    pallas_call x1, Pallas kernels, merge(): pl.pallas_call(lambda *refs: merge_kernel(fronts, subs, *refs), out_shape...  112 us
    unnamed x2, local copies, waits for them, and re-layouts  3.7 us

profile of v2, /device:TPU:11, one launch (start us, length us, event | category | flops | bytes accessed | tf_op | source)
XLA Modules:
  0.0 115.3 jit_solution(13238945228990174271)
XLA Ops:
  0.0 1.4 %copy.6.refs_1_ = s32[128,1]{1,0:T(8,128)} copy(s32[128,1]{0,1:T(1,128)} %param.6) | data formatting | bytes 1024 | tf_op args[1]
  1.4 111.6 %front_merge.1 = f32[256,1024]{1,0:T(8,128)} custom-call(f32[128,1024]{1,0:T(8,128)} %refs_0_.1, s32[128,1]{1,0:T(8,128)} %copy.6.refs_1_, f32[2,128,512]{2,1,0:T(8,128)} %refs_2_.1, s32[2,512]{1,0:T(2,128)} %refs_3_.1, f32[1,1024]{1,0:T(1,128)} %refs_4_.1), custom_call_target="tpu_custom_call" | custom-call | tf_op jit(solution)/shard_map/front_merge/pallas_call | solution.py:353
  113.0 2.3 %copy.8 = f32[1,256,1024]{2,1,0:T(8,128)} copy(f32[1,256,1024]{2,1,0:T(8,128)} %bitcast.1) | data formatting | bytes 2097152

commit v3 on v2

--- a/solution.py
+++ b/solution.py
@@ -89,6 +89,8 @@
     damping_ref,
     out_ref,
     slots,
+    away,
+    pairs,
     recv,
     children,
     zeros,
@@ -101,6 +103,8 @@
     block,
     upper,
     inverse,
+    pair_send,
+    pair_recv,
     send_sem,
     recv_sem,
     child_send,
@@ -152,7 +156,13 @@
 
     zeros[...] = jnp.zeros_like(zeros)
 
-    chosen = (dest_ref[...] == lax.broadcasted_iota(jnp.int32, (rows_held, fronts), 1)).astype(F32)
+    core = lax.rem(me, 2)
+    pair = me // 2
+    half = fronts // 2
+    place = lax.broadcasted_iota(jnp.int32, (rows_held, fronts), 1)
+    late = place >= half
+    name = jnp.where(late, 2 * (place - half) + (1 - core), 2 * place + core)
+    chosen = (dest_ref[...] == name).astype(F32)
     before = (
         lax.broadcasted_iota(jnp.int32, (rows_held, rows_held), 1)
         < lax.broadcasted_iota(jnp.int32, (rows_held, rows_held), 0)
@@ -164,22 +174,33 @@
         placed = mm(pick, parts[0], ROWS) + mm(pick, parts[1], ROWS)
         for k in range(per_row):
             slots[pl.ds(slot * per_row + k, fronts, stride=size), :] = placed[:, k * LANES : (k + 1) * LANES]
-
-    def piece(front):
-        return slots.at[pl.ds(pl.multiple_of(front * size, size), size), :]
-
-    steps = fronts // groups
+    for j in range(half):
+        pairs[j, :size, :] = slots[j * size : (j + 1) * size, :]
+        away[j] = slots[(half + j) * size : (half + j + 1) * size, :]
+
+    swap = pltpu.make_async_remote_copy(
+        src_ref=away,
+        dst_ref=pairs.at[:, size:, :],
+        send_sem=pair_send,
+        recv_sem=pair_recv,
+        device_id=(me + 1 - 2 * core, sub),
+        device_id_type=MESH,
+    )
+    swap.start()
+    swap.wait()
+    steps = half // groups
     for g in range(groups):
 
         def send(i, carry):
-            front = lax.rem(me + STRIDE * i, fronts)
+            to = lax.rem(pair + STRIDE * i, half)
+            front = 2 * to + core
             target = root_of(front)
 
             @pl.when((front != me) | (target != sub))
             def _():
                 pltpu.make_async_remote_copy(
-                    src_ref=piece(front),
-                    dst_ref=recv.at[pl.ds(pl.multiple_of((i * subs + sub) * size, size), size), :],
+                    src_ref=pairs.at[to],
+                    dst_ref=recv.at[pl.ds(pl.multiple_of((i * subs + sub) * 2 * size, 2 * size), 2 * size), :],
                     send_sem=send_sem,
                     recv_sem=recv_sem.at[g],
                     device_id=(front, target),
@@ -218,7 +239,7 @@
 
     @pl.when(sub == root)
     def _():
-        recv[pl.ds(pl.multiple_of(sub * size, size), size), :] = slots[pl.ds(pl.multiple_of(me * size, size), size), :]
+        recv[pl.ds(pl.multiple_of(sub * 2 * size, 2 * size), 2 * size), :] = pairs[pair]
         for s in range(subs):
 
             @pl.when(root == s)
@@ -248,7 +269,7 @@
             gram[c0:c1, c0:c1] += jnp.where(on_diagonal, weight * weight, 0.0)
 
         slots_in = steps * subs
-        count = 2 * slots_in
+        count = 4 * slots_in
 
         def gather(g, carry):
             for h in range(groups):
@@ -256,7 +277,7 @@
                 @pl.when(g == h)
                 def _():
                     first = 1 if h == 0 else 0
-                    region = recv.at[pl.ds(0, (slots_in - first) * size), :]
+                    region = recv.at[pl.ds(0, (slots_in - first) * 2 * size), :]
                     pltpu.make_async_copy(region, region, recv_sem.at[h]).wait()
 
             for q in range(count // BLOCK):
@@ -319,7 +340,7 @@
             def _():
                 row_keep(b).wait()
 
-        sent = slots.at[pl.ds(0, (fronts - 1) * size), :]
+        sent = pairs.at[pl.ds(0, half - 1)]
         pltpu.make_async_copy(sent, sent, send_sem).wait()
 
     @pl.when(sub != root)
@@ -332,7 +353,7 @@
                 for b in range(s * per_sub, (s + 1) * per_sub):
                     row_copy_out(b).wait_recv()
 
-        pltpu.make_async_copy(slots, slots, send_sem).wait()
+        pltpu.make_async_copy(pairs, pairs, send_sem).wait()
 
     for b in range(blocks):
         if b:
@@ -357,6 +378,8 @@
         out_specs=pl.BlockSpec(memory_space=pl.ANY),
         scratch_shapes=[
             pltpu.VMEM((fronts * size, LANES), F32),
+            pltpu.VMEM((fronts // 2, size, LANES), F32),
+            pltpu.VMEM((fronts // 2, 2 * size, LANES), F32),
             pltpu.VMEM((fronts * subs * size, LANES), F32),
             pltpu.VMEM((subs,) + child.shape, F32),
             pltpu.VMEM((BLOCK, width), F32),
@@ -370,6 +393,8 @@
             pltpu.VMEM((BLOCK, BLOCK), F32),
             pltpu.VMEM((BLOCK, BLOCK), F32),
             pltpu.SemaphoreType.DMA,
+            pltpu.SemaphoreType.DMA,
+            pltpu.SemaphoreType.DMA,
             pltpu.SemaphoreType.DMA((groups,)),
             pltpu.SemaphoreType.DMA,
             pltpu.SemaphoreType.DMA((subs,)),

time: 115 us -> 116 us (level)
  the two profiles are of different devices: /device:TPU:11 before, /device:TPU:20 now
where the time goes in v3:
time: 116 us
  Pallas kernels  112 us (97%)
  local copies, waits for them, and re-layouts  3.7 us (3%)
    pallas_call x1, Pallas kernels, merge(): pl.pallas_call(lambda *refs: merge_kernel(fronts, subs, *refs), out_shape...  112 us
    unnamed x2, local copies, waits for them, and re-layouts  3.7 us

profile of v3, /device:TPU:20, one launch (start us, length us, event | category | flops | bytes accessed | tf_op | source)
XLA Modules:
  0.0 115.6 jit_solution(10182282069093838611)
XLA Ops:
  0.0 1.4 %copy.6.refs_1_ = s32[128,1]{1,0:T(8,128)} copy(s32[128,1]{0,1:T(1,128)} %param.6) | data formatting | bytes 1024 | tf_op args[1]
  1.4 111.9 %front_merge.1 = f32[256,1024]{1,0:T(8,128)} custom-call(f32[128,1024]{1,0:T(8,128)} %refs_0_.1, s32[128,1]{1,0:T(8,128)} %copy.6.refs_1_, f32[2,128,512]{2,1,0:T(8,128)} %refs_2_.1, s32[2,512]{1,0:T(2,128)} %refs_3_.1, f32[1,1024]{1,0:T(1,128)} %refs_4_.1), custom_call_target="tpu_custom_call" | custom-call | tf_op jit(solution)/shard_map/front_merge/pallas_call | solution.py:374
  113.3 2.3 %copy.8 = f32[1,256,1024]{2,1,0:T(8,128)} copy(f32[1,256,1024]{2,1,0:T(8,128)} %bitcast.1) | data formatting | bytes 2097152

commit v4 on v2

v4 whole, which is shorter than its diff:
```python
import jax
import jax.numpy as jnp
from jax import lax
from jax.experimental import pallas as pl
from jax.experimental.pallas import tpu as pltpu
from jax.sharding import PartitionSpec as P

F32 = jnp.float32
BF16 = jnp.bfloat16
BLOCK = 128
LANES = 128
GROUP = 8
GROUPS = 4
STRIDE = 53
CUTS = (0, 4, 8)
MESH = pl.DeviceIdType.MESH
KEEP = (((1,), (0,)), ((), ()))
ROWS = (((0,), (0,)), ((), ()))
COLS = (((1,), (1,)), ((), ()))


def mm(left, right, dims):
    return lax.dot_general(left, right, dims, preferred_element_type=F32)


def split(x):
    high = x.astype(BF16)
    return high, (x - high.astype(F32)).astype(BF16)


def mm3(left, right, dims):
    return mm(left[0], right[0], dims) + (mm(left[0], right[1], dims) + mm(left[1], right[0], dims))


def root_of(front):
    return lax.rem(2 * (front % 2) + (front // 2) % 2 + front // 4 + front // 16, 4)


def lane_copy(x, j):
    return jnp.broadcast_to(x[:, j : j + 1], (GROUP, LANES))


def row_copy(x, j):
    return jnp.broadcast_to(x[j : j + 1, :], (GROUP, LANES))


def factor_block(source, upper_ref, inverse_ref):
    count = BLOCK // GROUP
    sub = lax.broadcasted_iota(jnp.int32, (GROUP, LANES), 0)
    lane = lax.broadcasted_iota(jnp.int32, (GROUP, LANES), 1)
    a = [source[GROUP * k : GROUP * (k + 1), :] for k in range(count)]
    e = [jnp.where(lane == sub + GROUP * k, 1.0, 0.0).astype(F32) for k in range(count)]
    zero = 0.0 * a[0]
    for k in range(count):
        b = [lane_copy(a[k], GROUP * k + m) + zero for m in range(GROUP)]
        more = k + 1 < count
        c = [lane_copy(a[k + 1], GROUP * k + m) for m in range(GROUP)] if more else None
        pivots = None
        for j in range(GROUP):
            pivot = row_copy(b[j], j)
            pivots = pivot if pivots is None else jnp.where(sub >= j, pivot, pivots)
            inv = 1.0 / pivot
            ratio = jnp.where(sub > j, b[j], 0.0) * inv
            below = c[j] * inv if more else None
            for m in range(j + 1, GROUP):
                u = row_copy(b[m], j)
                b[m] = b[m] - ratio * u
                if more:
                    c[m] = c[m] - below * u
            row_a, row_e = row_copy(a[k], j), row_copy(e[k], j)
            a[k] = a[k] - ratio * row_a
            e[k] = e[k] - ratio * row_e
            if more:
                a[k + 1] = a[k + 1] - below * row_a
                e[k + 1] = e[k + 1] - below * row_e
        scale = lax.rsqrt(pivots)
        top, side = a[k] * scale, e[k] * scale
        upper_ref[GROUP * k : GROUP * (k + 1), :] = top
        inverse_ref[GROUP * k : GROUP * (k + 1), :] = side
        if k + 2 < count:
            both = jnp.concatenate([top, side], axis=1)
            high = both.astype(BF16).astype(F32)
            low = both - high
            change = mm3((high[:, :LANES], low[:, :LANES]), (high, low), ROWS)
            for q in range(k + 2, count):
                a[q] = a[q] - change[GROUP * q : GROUP * (q + 1), :LANES]
                e[q] = e[q] - change[GROUP * q : GROUP * (q + 1), LANES:]


def merge_kernel(
    fronts,
    subs,
    rows_ref,
    dest_ref,
    child_ref,
    columns_ref,
    damping_ref,
    out_ref,
    slots,
    away,
    pairs,
    recv,
    children,
    zeros,
    kh,
    kl,
    xh,
    xl,
    gram,
    r_full,
    rh,
    rl,
    lh,
    ll,
    block,
    upper,
    inverse,
    pair_send,
    pair_recv,
    send_sem,
    recv_sem,
    child_send,
    child_recv,
    child_own,
    fill_sem,
    row_send,
    row_recv,
):
    me = lax.axis_index("front")
    sub = lax.axis_index("sub")
    root = root_of(me)
    rows_held, width = rows_ref.shape
    kids, _, contrib = child_ref.shape
    groups = recv_sem.shape[1]
    blocks = width // BLOCK
    per_sub = blocks // subs
    parts = len(CUTS) - 1
    wide = CUTS[1] - CUTS[0]
    size = 2 * wide

    def child_copy(s):
        return pltpu.make_async_remote_copy(
            src_ref=child_ref.at[:, :, s * BLOCK :],
            dst_ref=children.at[s, :, :, s * BLOCK :],
            send_sem=child_send,
            recv_sem=child_recv.at[s],
            device_id=(me, root),
            device_id_type=MESH,
        )

    def child_keep(s):
        return pltpu.make_async_copy(child_ref.at[:, :, s * BLOCK :], children.at[s, :, :, s * BLOCK :], child_own)

    for s in range(subs):

        @pl.when((sub == s) & (root != s))
        def _():
            child_copy(s).start()

        @pl.when((sub == s) & (root == s))
        def _():
            child_keep(s).start()

    def fill(b):
        half = b % per_sub
        return pltpu.make_async_copy(
            zeros.at[:, : b * BLOCK], out_ref.at[half * BLOCK : (half + 1) * BLOCK, : b * BLOCK], fill_sem.at[half]
        )

    zeros[...] = jnp.zeros_like(zeros)

    core = lax.rem(me, 2)
    pair = me // 2
    half = fronts // 2
    place = lax.broadcasted_iota(jnp.int32, (rows_held, fronts), 1)
    late = place >= half
    name = jnp.where(late, 2 * (place - half) + (1 - core), 2 * place + core)
    chosen = (dest_ref[...] == name).astype(F32)
    before = (
        lax.broadcasted_iota(jnp.int32, (rows_held, rows_held), 1)
        < lax.broadcasted_iota(jnp.int32, (rows_held, rows_held), 0)
    ).astype(BF16)
    earlier = mm(before, chosen.astype(BF16), KEEP)
    pieces = split(rows_ref[...])
    for slot in range(2):
        pick = jnp.where(earlier == slot, chosen, 0.0).astype(BF16)
        placed = mm(pick, pieces[0], ROWS) + mm(pick, pieces[1], ROWS)
        for p in range(parts):
            for k in range(wide):
                at = (CUTS[p] + k) * LANES
                slots[pl.ds(p * fronts * size + slot * wide + k, fronts, stride=size), :] = placed[:, at : at + LANES]
    for p in range(parts):
        for j in range(half):
            at = (p * fronts + j) * size
            pairs[p, j, :size, :] = slots[at : at + size, :]
            away[p, j] = slots[at + half * size : at + (half + 1) * size, :]

    def swap(p):
        return pltpu.make_async_remote_copy(
            src_ref=away.at[p],
            dst_ref=pairs.at[p, :, size:, :],
            send_sem=pair_send.at[p],
            recv_sem=pair_recv.at[p],
            device_id=(me + 1 - 2 * core, sub),
            device_id_type=MESH,
        )

    for p in range(parts):
        swap(p).start()
    steps = half // groups
    for p in range(parts):
        swap(p).wait()
        for g in range(groups):

            def send(i, carry):
                to = lax.rem(pair + STRIDE * i, half)
                front = 2 * to + core
                target = root_of(front)

                @pl.when((front != me) | (target != sub))
                def _():
                    pltpu.make_async_remote_copy(
                        src_ref=pairs.at[p, to],
                        dst_ref=recv.at[
                            pl.ds(pl.multiple_of(((p * half + i) * subs + sub) * 2 * size, 2 * size), 2 * size), :
                        ],
                        send_sem=send_sem.at[p],
                        recv_sem=recv_sem.at[p, g],
                        device_id=(front, target),
                        device_id_type=MESH,
                    ).start()

                return carry

            lax.fori_loop(g * steps, (g + 1) * steps, send, 0)

    for b in range(blocks):
        if b:

            @pl.when(sub == b // per_sub)
            def _():
                fill(b).start()

    def part_of(b):
        return [p for p in range(parts) if CUTS[p + 1] > b]

    def row_piece(b, p):
        half = b % per_sub
        lo, hi = max(b, CUTS[p]) * BLOCK, CUTS[p + 1] * BLOCK
        return r_full.at[b * BLOCK : (b + 1) * BLOCK, lo:hi], out_ref.at[half * BLOCK : (half + 1) * BLOCK, lo:hi]

    def row_copy_out(b, p):
        src, dst = row_piece(b, p)
        return pltpu.make_async_remote_copy(
            src_ref=src,
            dst_ref=dst,
            send_sem=row_send.at[b, p],
            recv_sem=row_recv.at[b % per_sub, p],
            device_id=(me, b // per_sub),
            device_id_type=MESH,
        )

    def row_keep(b, p):
        src, dst = row_piece(b, p)
        return pltpu.make_async_copy(src, dst, row_send.at[b, p])

    def row_out(b, p):
        @pl.when(root != b // per_sub)
        def _():
            row_copy_out(b, p).start()

        @pl.when(root == b // per_sub)
        def _():
            row_keep(b, p).start()

    @pl.when(sub == root)
    def _():
        for p in range(parts):
            recv[pl.ds(pl.multiple_of((p * half * subs + sub) * 2 * size, 2 * size), 2 * size), :] = pairs[p, pair]
        for s in range(subs):

            @pl.when(root == s)
            def _():
                child_keep(s).wait()

            @pl.when(root != s)
            def _():
                child_copy(s).wait_recv()

        for c in range(kids):
            spread = (
                lax.broadcasted_iota(jnp.int32, (width, contrib), 0) == columns_ref[c : c + 1, :]
            ).astype(F32).astype(BF16)
            for s in range(subs):
                high, low = split(children[s, c, :, s * BLOCK :])
                at = c * contrib + s * BLOCK
                kh[at : at + BLOCK, :] = mm(high, spread[:, s * BLOCK :], COLS).astype(BF16)
                kl[at : at + BLOCK, :] = mm(low, spread[:, s * BLOCK :], COLS).astype(BF16)
        on_diagonal = lax.broadcasted_iota(jnp.int32, (BLOCK, BLOCK), 0) == lax.broadcasted_iota(
            jnp.int32, (BLOCK, BLOCK), 1
        )
        count = 4 * steps * subs

        def columns_in(p):
            end = CUTS[p + 1] * BLOCK
            for b in range(CUTS[p + 1]):
                c0, c1 = b * BLOCK, (b + 1) * BLOCK
                lo = max(b, CUTS[p]) * BLOCK
                gram[c0:c1, lo:end] = mm3((kh[:, c0:c1], kl[:, c0:c1]), (kh[:, lo:end], kl[:, lo:end]), ROWS)
                if b >= CUTS[p]:
                    weight = damping_ref[:, c0:c1]
                    gram[c0:c1, c0:c1] += jnp.where(on_diagonal, weight * weight, 0.0)

            def gather(g, carry):
                for h in range(groups):

                    @pl.when(g == h)
                    def _():
                        first = 1 if h == 0 else 0
                        region = recv.at[pl.ds(0, (steps * subs - first) * 2 * size), :]
                        pltpu.make_async_copy(region, region, recv_sem.at[p, h]).wait()

                for q in range(count // BLOCK):
                    base = pl.multiple_of(g * count + q * BLOCK, BLOCK)
                    first = p * half * subs * 2 * size
                    for k in range(wide):
                        at = (CUTS[p] + k) * LANES
                        high, low = split(recv[pl.ds(first + base * wide + k, BLOCK, stride=wide), :])
                        xh[pl.ds(base, BLOCK), at : at + LANES] = high
                        xl[pl.ds(base, BLOCK), at : at + LANES] = low
                here = pl.ds(pl.multiple_of(g * count, count), count)
                for b in range(CUTS[p + 1]):
                    c0, c1 = b * BLOCK, (b + 1) * BLOCK
                    lo = max(b, CUTS[p]) * BLOCK
                    gram[c0:c1, lo:end] += mm3(
                        (xh[here, c0:c1], xl[here, c0:c1]), (xh[here, lo:end], xl[here, lo:end]), ROWS
                    )
                return carry

            lax.fori_loop(0, groups, gather, 0)

        def finish(b, lo, hi, inverse_parts):
            c0, c1 = b * BLOCK, (b + 1) * BLOCK
            rest = mm3(inverse_parts, split(gram[c0:c1, lo:hi]), KEEP)
            r_full[c0:c1, lo:hi] = rest
            rh[c0:c1, lo:hi], rl[c0:c1, lo:hi] = split(rest)

        def reduce(b, lo, hi):
            c0, c1 = b * BLOCK, (b + 1) * BLOCK
            gram[c0:c1, lo:hi] -= mm3((rh[:c0, c0:c1], rl[:c0, c0:c1]), (rh[:c0, lo:hi], rl[:c0, lo:hi]), ROWS)

        def step(i, carry):
            for p in range(parts):
                for b in range(CUTS[p], CUTS[p + 1]):

                    @pl.when(i == b)
                    def _():
                        lo, hi = CUTS[p] * BLOCK, CUTS[p + 1] * BLOCK
                        c0, c1 = b * BLOCK, (b + 1) * BLOCK
                        if b == CUTS[p]:
                            columns_in(p)
                            for q in range(b):
                                if q:
                                    reduce(q, lo, hi)
                                at = slice(q * BLOCK, (q + 1) * BLOCK)
                                finish(q, lo, hi, (lh[at, :], ll[at, :]))
                                row_out(q, p)
                        if b:
                            reduce(b, c0, hi)
                        block[...] = gram[c0:c1, c0:c1]

            factor_block(block, upper, inverse)
            for p in range(parts):
                for b in range(CUTS[p], CUTS[p + 1]):

                    @pl.when(i == b)
                    def _():
                        hi = CUTS[p + 1] * BLOCK
                        c0, c1 = b * BLOCK, (b + 1) * BLOCK
                        r_full[c0:c1, c0:c1] = upper[...]
                        solve = split(inverse[...])
                        if p + 1 < parts:
                            lh[c0:c1, :], ll[c0:c1, :] = solve
                        if c1 < hi:
                            finish(b, c1, hi, solve)
                        row_out(b, p)

            return carry

        lax.fori_loop(0, blocks, step, 0)
        for b in range(blocks):
            for p in part_of(b):

                @pl.when(root != b // per_sub)
                def _():
                    row_copy_out(b, p).wait_send()

                @pl.when(root == b // per_sub)
                def _():
                    row_keep(b, p).wait()

        for p in range(parts):
            sent = pairs.at[p, pl.ds(0, half - 1)]
            pltpu.make_async_copy(sent, sent, send_sem.at[p]).wait()

    @pl.when(sub != root)
    def _():
        for s in range(subs):

            @pl.when(sub == s)
            def _():
                child_copy(s).wait_send()
                for b in range(s * per_sub, (s + 1) * per_sub):
                    for p in part_of(b):
                        row_copy_out(b, p).wait_recv()

        for p in range(parts):
            pltpu.make_async_copy(pairs.at[p], pairs.at[p], send_sem.at[p]).wait()

    for b in range(blocks):
        if b:

            @pl.when(sub == b // per_sub)
            def _():
                fill(b).wait()


def merge(rows, dest, child, columns, damping, fronts, subs):
    rows_held, width = rows.shape
    parts = len(CUTS) - 1
    size = 2 * (CUTS[1] - CUTS[0])
    kids, _, contrib = child.shape
    blocks = width // BLOCK
    half = fronts // 2
    solved = CUTS[-2] * BLOCK
    vmem = pl.BlockSpec(memory_space=pltpu.VMEM)
    return pl.pallas_call(
        lambda *refs: merge_kernel(fronts, subs, *refs),
        out_shape=jax.ShapeDtypeStruct((width // subs, width), F32),
        in_specs=[vmem, vmem, pl.BlockSpec(memory_space=pl.ANY), vmem, vmem],
        out_specs=pl.BlockSpec(memory_space=pl.ANY),
        scratch_shapes=[
            pltpu.VMEM((parts * fronts * size, LANES), F32),
            pltpu.VMEM((parts, half, size, LANES), F32),
            pltpu.VMEM((parts, half, 2 * size, LANES), F32),
            pltpu.VMEM((parts * half * subs * 2 * size, LANES), F32),
            pltpu.VMEM((subs,) + child.shape, F32),
            pltpu.VMEM((BLOCK, width), F32),
            pltpu.VMEM((kids * contrib, width), BF16),
            pltpu.VMEM((kids * contrib, width), BF16),
            pltpu.VMEM((2 * fronts * subs, width), BF16),
            pltpu.VMEM((2 * fronts * subs, width), BF16),
            pltpu.VMEM((width, width), F32),
            pltpu.VMEM((width, width), F32),
            pltpu.VMEM((width, width), BF16),
            pltpu.VMEM((width, width), BF16),
            pltpu.VMEM((solved, BLOCK), BF16),
            pltpu.VMEM((solved, BLOCK), BF16),
            pltpu.VMEM((BLOCK, BLOCK), F32),
            pltpu.VMEM((BLOCK, BLOCK), F32),
            pltpu.VMEM((BLOCK, BLOCK), F32),
            pltpu.SemaphoreType.DMA((parts,)),
            pltpu.SemaphoreType.DMA((parts,)),
            pltpu.SemaphoreType.DMA((parts,)),
            pltpu.SemaphoreType.DMA((parts, GROUPS)),
            pltpu.SemaphoreType.DMA,
            pltpu.SemaphoreType.DMA((subs,)),
            pltpu.SemaphoreType.DMA,
            pltpu.SemaphoreType.DMA((blocks // subs,)),
            pltpu.SemaphoreType.DMA((blocks, parts)),
            pltpu.SemaphoreType.DMA((blocks // subs, parts)),
        ],
        compiler_params=pltpu.CompilerParams(has_side_effects=True),
        name="front_merge",
    )(rows, dest, child, columns, damping)


def local(row_values, front_of_row, child_factors, child_columns, damping):
    fronts = lax.axis_size("front")
    subs = lax.axis_size("sub")
    return merge(row_values, front_of_row, child_factors, child_columns, damping, fronts, subs)[None]


def solution(mesh):
    in_specs = (
        P(("front", "sub"), None),
        P(("front", "sub"), None),
        P("front", "sub", None),
        P("front", None),
        P("front", None),
    )
    out_specs = P("front", "sub", None)
    return jax.shard_map(local, mesh=mesh, in_specs=in_specs, out_specs=out_specs, check_vma=False)
```

time: 115 us -> 118 us (1.026)
  the two profiles are of different devices: /device:TPU:11 before, /device:TPU:32 now
where the time goes in v4:
time: 118 us
  Pallas kernels  114 us (97%)
  local copies, waits for them, and re-layouts  3.7 us (3%)
    pallas_call x1, Pallas kernels, merge(): pl.pallas_call(lambda *refs: merge_kernel(fronts, subs, *refs), out_shape...  114 us
    unnamed x2, local copies, waits for them, and re-layouts  3.7 us

profile of v4, /device:TPU:32, one launch (start us, length us, event | category | flops | bytes accessed | tf_op | source)
XLA Modules:
  0.0 118.2 jit_solution(2972212554605352338)
XLA Ops:
  0.0 1.4 %copy.6.refs_1_ = s32[128,1]{1,0:T(8,128)} copy(s32[128,1]{0,1:T(1,128)} %param.6) | data formatting | bytes 1024 | tf_op args[1]
  1.4 114.5 %front_merge.1 = f32[256,1024]{1,0:T(8,128)} custom-call(f32[128,1024]{1,0:T(8,128)} %refs_0_.1, s32[128,1]{1,0:T(8,128)} %copy.6.refs_1_, f32[2,128,512]{2,1,0:T(8,128)} %refs_2_.1, s32[2,512]{1,0:T(2,128)} %refs_3_.1, f32[1,1024]{1,0:T(1,128)} %refs_4_.1), custom_call_target="tpu_custom_call" | custom-call | tf_op jit(solution)/shard_map/front_merge/pallas_call | solution.py:437
  115.9 2.3 %copy.8 = f32[1,256,1024]{2,1,0:T(8,128)} copy(f32[1,256,1024]{2,1,0:T(8,128)} %bitcast.1) | data formatting | bytes 2097152
